TPU v7x, 32 devices: a whole 2x2x4 slice. The times are simulated.
32 devices in a mesh: occ: 8 (over z, core), aux: 4 (over y, x).
Axes of the slice: x: 2, y: 2, z: 4, core: 2. Of those that a mesh axis runs over, the one named last changes fastest.
Arguments:
- integrals: bfloat16 [2048, 256, 512], P('aux', 'occ'), may hold values from -1.1953125 to 1.1953125
- metric: bfloat16 [2048, 2048], replicated, may hold values from -0.125 to 0.125
- e_occ: float32 [256], replicated, may hold values from -2 to -0.3
- e_vir: float32 [512], replicated, may hold values from 0.2 to 3
- partner: int32 [256, 2], P(('occ', 'aux')), may hold values from 0 to 7
- screen: int32 [256, 2], P(('occ', 'aux')), may hold values from 0 to 1
Outputs:
- gradient: bfloat16 [2048, 256, 512], P(None, ('occ', 'aux'))
- density: float32 [512, 512], P('occ')
All inputs are finite; a program needn't handle non-finite values.
Results may differ from a plain program's by a relative error of at most 0.0055.
Values may be sent and summed in bfloat16 or wider, within the bound.
A program may use at most 192 MiB of HBM per device.

v0:
```python
import jax
import jax.numpy as jnp
from jax import lax
from jax.sharding import PartitionSpec as P

NOCC = 256
ROUNDS = 2


def passed_along(array, axis, by):
    count = lax.axis_size(axis)
    return lax.ppermute(array, axis, [(i, (i + by) % count) for i in range(count)])


def transform(metric, moved):
    shape = moved.shape
    mixed = jnp.dot(metric, moved.reshape(shape[0], -1), preferred_element_type=jnp.float32)
    return mixed.astype(jnp.bfloat16).reshape(shape)


def fetch_block(coeff, offset):
    return passed_along(coeff, ("occ", "aux"), offset)


def on_device(integrals, metric, e_occ, e_vir, partner, screen):
    groups = lax.axis_size(("occ", "aux"))
    moved = lax.all_to_all(integrals, "aux", split_axis=1, concat_axis=0, tiled=True)
    coeff = transform(metric, moved)
    naux, own, nvir = coeff.shape
    device = lax.axis_index(("occ", "aux"))
    pair_sum = e_vir[:, None] + e_vir[None, :]
    gamma = jnp.zeros((naux, own, nvir), jnp.float32)
    density = jnp.zeros((nvir, nvir), jnp.float32)
    shifts = (1, groups // 2)
    for rnd in range(ROUNDS):
        offset = shifts[rnd % 2]
        fetched = fetch_block(coeff, offset)
        source = (device - offset) % groups

        def one_pair(carry, slot, rnd=rnd, fetched=fetched, source=source):
            grad_acc, dens_acc = carry
            local = partner[slot, rnd]
            kept = screen[slot, rnd].astype(jnp.float32)
            left = lax.dynamic_index_in_dim(coeff, slot, 1, False)
            right = lax.dynamic_index_in_dim(fetched, local, 1, False)
            intersection = lax.dot_general(
                left, right, (((0,), (0,)), ((), ())), preferred_element_type=jnp.float32
            )
            gap = pair_sum - e_occ[device * own + slot] - e_occ[source * own + local]
            amp = (kept * intersection / gap).astype(jnp.bfloat16)
            term = lax.dot_general(
                right, amp, (((1,), (1,)), ((), ())), preferred_element_type=jnp.float32
            )
            column = lax.dynamic_index_in_dim(grad_acc, slot, 1, False) + term
            grad_acc = lax.dynamic_update_index_in_dim(grad_acc, column, slot, 1)
            dens_acc = dens_acc + lax.dot_general(
                amp, amp, (((1,), (1,)), ((), ())), preferred_element_type=jnp.float32
            )
            return (grad_acc, dens_acc)

        def visit(slot, carry, rnd=rnd, one_pair=one_pair):
            return one_pair(carry, slot)

        gamma, density = lax.fori_loop(0, own, visit, (gamma, density))
    total = lax.psum(density, ("occ", "aux"))
    height = nvir // lax.axis_size("occ")
    block = lax.dynamic_slice_in_dim(total, lax.axis_index("occ") * height, height, 0)
    return (gamma.astype(jnp.bfloat16), block / NOCC)


def solution(mesh):
    placed = (
        P("aux", "occ", None),
        P(),
        P(),
        P(),
        P(("occ", "aux"), None),
        P(("occ", "aux"), None),
    )
    return jax.shard_map(
        on_device,
        mesh=mesh,
        in_specs=placed,
        out_specs=(P(None, ("occ", "aux"), None), P("occ", None)),
        check_vma=False,
    )
```

profile of v0, /device:TPU:0, one launch (start us, length us, event | category | flops | bytes accessed | tf_op | source)
XLA Modules:
  0.0 1485.5 jit_solution(9783774959772987957)
XLA Ops:
  7.2 12.0 copy.15
  19.3 187.7 %all_to_all.15 = bf16[512,32,512]{2,0,1:T(8,128)(2,1)S(1)} all-to-all(bf16[512,32,512]{2,0,1:T(8,128)(2,1)S(1)} %copy.15), channel_id=1, replica_groups=mesh['occ'=8,'aux'=4] {'aux'}, dimensions={1} | all-to-all | bytes 33554432 | tf_op jit(solution)/shard_map/all_to_all | solution.py:27
  206.9 38.4 %copy.16 = bf16[512,4,8,512]{3,2,0,1:T(8,128)(2,1)S(1)} copy(bf16[512,4,8,512]{3,0,2,1:T(8,128)(2,1)S(1)} %bitcast.109) | data formatting | bytes 33554432 | tf_op jit(solution)/shard_map/all_to_all | solution.py:27
  245.4 10.5 copy.23
  255.9 38.5 %convolution_convert_fusion = bf16[2048,4096]{1,0:T(8,128)(2,1)S(1)} fusion(bf16[2048,2048]{1,0:T(8,128)(2,1)S(1)} %bitcast.114, bf16[2048,4096]{1,0:T(8,128)(2,1)} %bitcast.111), kind=kOutput, calls=%fused_computation.42 | convolution fusion | flops 34368126976 | bytes 41943040 | tf_op jit(solution)/shard_map/dot_general | solution.py:17
  294.4 7.4 copy.27
  305.4 362.3 %collective-permute-done = bf16[2048,8,512]{2,0,1:T(8,128)(2,1)} collective-permute-done((bf16[2048,8,512]{2,0,1:T(8,128)(2,1)}, bf16[2048,8,512]{2,0,1:T(8,128)(2,1)}, u32[]{:S(2)}, u32[]{:S(2)}) %collective-permute-start) | collective-permute-done | bytes 16777248 | tf_op jit(solution)/shard_map/ppermute | solution.py:12
  667.7 11.3 broadcast_in_dim.27
  679.0 138.9 %while.37 = (s32[]{:T(128)}, f32[2048,8,512]{2,0,1:T(8,128)}, f32[512,512]{1,0:T(8,128)S(1)}, s32[8,2]{0,1:T(2,128)S(1)}, bf16[2048,8,512]{2,0,1:T(8,128)(2,1)},...) while((s32[]{:T(128)}, f32[2048,8,512]{2,0,1:T(8,128)}, ...), condition=%wide.region_1.2_spmd.clone, body=%wide.region_0.1_spmd.clone.sunk | while | flops 2419064832 | bytes 26745676 | solution.py:64
  682.8 5.4 fusion.79
  688.2 2.6 constant_dynamic-slice_fusion.12
  690.8 4.9 bitcast_dynamic-update-slice_fusion.5
  700.1 5.4 fusion.79
  708.2 4.9 bitcast_dynamic-update-slice_fusion.5
  717.5 5.4 fusion.79
  722.9 2.6 constant_dynamic-slice_fusion.12
  725.6 4.9 bitcast_dynamic-update-slice_fusion.5
  734.9 5.4 fusion.79
  740.3 2.6 constant_dynamic-slice_fusion.12
  742.9 4.9 bitcast_dynamic-update-slice_fusion.5
  752.2 5.4 fusion.79
  760.3 4.9 bitcast_dynamic-update-slice_fusion.5
  769.6 5.4 fusion.79
  777.6 4.9 bitcast_dynamic-update-slice_fusion.5
  787.0 5.4 fusion.79
  795.0 4.9 bitcast_dynamic-update-slice_fusion.5
  804.3 5.4 fusion.79
  812.4 4.9 bitcast_dynamic-update-slice_fusion.5
  817.9 206.2 %collective-permute-done.1 = bf16[2048,8,512]{2,0,1:T(8,128)(2,1)} collective-permute-done((bf16[2048,8,512]{2,0,1:T(8,128)(2,1)}, bf16[2048,8,512]{2,0,1:T(8,128)(2,1)}, u32[]{:S(2)}, u32[]{:S(2)}) %collective-permute-start.1) | collective-permute-done | bytes 16777248 | tf_op jit(solution)/shard_map/ppermute | solution.py:12
  1024.1 140.7 %while.36 = (s32[]{:T(128)}, f32[2048,8,512]{2,0,1:T(8,128)}, f32[512,512]{1,0:T(8,128)S(1)}, s32[8,2]{0,1:T(2,128)S(1)}, bf16[2048,8,512]{2,0,1:T(8,128)(2,1)},...) while((s32[]{:T(128)}, f32[2048,8,512]{2,0,1:T(8,128)}, ...), condition=%wide.region_3.4_spmd.clone, body=%wide.region_2.3_spmd.clone.sunk | while | flops 2418802688 | bytes 26745668 | solution.py:64
  1028.2 5.4 fusion.71
  1036.3 4.9 bitcast_dynamic-update-slice_fusion.4
  1045.8 5.4 fusion.71
  1053.9 4.9 bitcast_dynamic-update-slice_fusion.4
  1063.4 5.4 fusion.71
  1071.5 4.9 bitcast_dynamic-update-slice_fusion.4
  1081.0 5.4 fusion.71
  1089.1 4.9 bitcast_dynamic-update-slice_fusion.4
  1098.6 5.4 fusion.71
  1106.6 4.9 bitcast_dynamic-update-slice_fusion.4
  1116.2 5.4 fusion.71
  1124.2 4.9 bitcast_dynamic-update-slice_fusion.4
  1133.8 5.4 fusion.71
  1141.8 4.9 bitcast_dynamic-update-slice_fusion.4
  1151.4 5.4 fusion.71
  1159.4 4.9 bitcast_dynamic-update-slice_fusion.4
  1165.8 31.3 %copy.26 = bf16[2048,8,512]{2,1,0:T(8,128)(2,1)} copy(f32[2048,8,512]{2,0,1:T(8,128)} %get-tuple-element.518) | data formatting | bytes 50331648 | tf_op jit(solution)/shard_map/while | solution.py:64
  1197.1 280.0 %all-reduce.2.cloned.1.call-done = f32[512,512]{1,0:T(8,128)} async-done(((f32[512,512]{1,0:T(8,128)}), f32[512,512]{1,0:T(8,128)}) %all-reduce.2.cloned.1.call-update) | async-done | bytes 1048592 | tf_op jit(solution)/shard_map/psum | solution.py:65
  (82 shorter events, 70.2 us)
Async XLA Ops:
  7.2 1469.9 %all-reduce.2.cloned.1.call-start = ((), (), s32[]{:S(2)}) async-start(), calls=%async_computation.1 | async-start | bytes 2097152 | tf_op jit(solution)/shard_map/psum | solution.py:65
  206.9 49.0 %slice-start = ((s8[8388608]{0:T(1024)(128)(4,1)}), s8[4194304]{0:T(1024)(128)(4,1)S(1)}, s32[]{:S(2)}) async-start(s8[8388608]{0:T(1024)(128)(4,1)} %bitcast.113), calls=%async_computation.2 | async-start | bytes 8388608
  245.3 10.5 slice-start.1
  301.9 365.8 %collective-permute-start = (bf16[2048,8,512]{2,0,1:T(8,128)(2,1)}, bf16[2048,8,512]{2,0,1:T(8,128)(2,1)}, u32[]{:S(2)}, u32[]{:S(2)}) collective-permute-start(bf16[2048,8,512]{2,0,1:T(8,128)(2,1)} %bitcast.60), channel_id=1, source_target_pairs={{0,1},{1,2},{2,3},{3,4},{4,5},{5,6},{6,7},{7,8},{8,9},{9,10},{10,1... | collective-permute-start | bytes 50331656 | tf_op jit(solution)/shard_map/ppermute | solution.py:12
  302.8 721.3 %collective-permute-start.1 = (bf16[2048,8,512]{2,0,1:T(8,128)(2,1)}, bf16[2048,8,512]{2,0,1:T(8,128)(2,1)}, u32[]{:S(2)}, u32[]{:S(2)}) collective-permute-start(bf16[2048,8,512]{2,0,1:T(8,128)(2,1)} %bitcast.60), channel_id=1, source_target_pairs={{0,16},{1,17},{2,18},{3,19},{4,20},{5,21},{6,22},{7,23},{8,24},{9,... | collective-permute-start | bytes 50331656 | tf_op jit(solution)/shard_map/ppermute | solution.py:12
  305.4 373.5 %copy-start.1 = (f32[256]{0:T(256)S(1)}, f32[256]{0:T(256)}, u32[]{:S(2)}) copy-start(f32[256]{0:T(256)} %param.12) | copy-start | bytes 3076
  305.4 373.6 %copy-start.2 = (s32[8,2]{0,1:T(2,128)S(1)}, s32[8,2]{0,1:T(2,128)}, u32[]{:S(2)}) copy-start(s32[8,2]{0,1:T(2,128)} %param.14) | copy-start | bytes 196
  305.4 373.6 %copy-start.3 = (s32[8,2]{0,1:T(2,128)S(1)}, s32[8,2]{0,1:T(2,128)}, u32[]{:S(2)}) copy-start(s32[8,2]{0,1:T(2,128)} %param.15) | copy-start | bytes 196
  305.4 373.6 %copy-start.4 = (f32[512]{0:T(512)S(1)}, f32[512]{0:T(512)}, u32[]{:S(2)}) copy-start(f32[512]{0:T(512)} %param.13) | copy-start | bytes 6148
  1164.8 1.0 copy-start
Sparse Core Ops, SparseCore 0:
  1165.9 311.0 all-reduce.1
where the time goes:
time: 1490 us
  waiting for transfers between devices  848 us (57%)
  matrix products  212 us (14%)
  blocking collectives  188 us (13%)
  local copies, waits for them, and re-layouts  165 us (11%)
  loops' own time  42.8 us (3%)
    ppermute x2, waiting for transfers between devices, passed_along(): lax.ppermute(array, axis, [(i, (i + by) % count) for i in range(count)])  568 us
    psum x1, waiting for transfers between devices, on_device(): total = lax.psum(density, ('occ', 'aux'))  280 us
    all_to_all x1, blocking collectives, on_device(): lax.all_to_all(integrals, 'aux', split_axis=1, concat_axis=0, tiled=True)  188 us
    dot_general x16, matrix products, one_pair(): lax.dot_general(left, right, (((0,), (0,)), ((), ())), preferred_element_...  86.2 us
    dot_general x16, matrix products, one_pair(): lax.dot_general(right, amp, (((1,), (1,)), ((), ())), preferred_element_t...  78.6 us
    another operation x2, loops' own time, on_device(): gamma, density = lax.fori_loop(0, own, visit, (gamma, density))  42.8 us
    dynamic_slice x16, local copies, waits for them, and re-layouts, one_pair(): column = lax.dynamic_index_in_dim(grad_acc, slot, 1, False) + term  42.2 us
    dot_general x1, matrix products, transform(): jnp.dot(metric, moved.reshape(shape[0], -1), preferred_element_type=jnp.f...  38.5 us
  transfers between devices with their start and end apart: 3, of which 3 were waited for; matrix products, arithmetic and copies ran while one was open for 11% of the time, Pallas kernels for 0%

commit v1 on v0

--- a/solution.py
+++ b/solution.py
@@ -62,7 +62,7 @@
             return one_pair(carry, slot)
 
         gamma, density = lax.fori_loop(0, own, visit, (gamma, density))
-    total = lax.psum(density, ("occ", "aux"))
+    total = jnp.sum(lax.all_gather(density, ("occ", "aux")), axis=0)
     height = nvir // lax.axis_size("occ")
     block = lax.dynamic_slice_in_dim(total, lax.axis_index("occ") * height, height, 0)
     return (gamma.astype(jnp.bfloat16), block / NOCC)

time: 1490 us -> 1560 us (1.047)
  waiting for transfers between devices: 848 us -> 913 us
    all_gather x0 -> x1, waiting for transfers between devices: none -> 343 us  [on_device(): total = jnp.sum(lax.all_gather(density, ('occ', 'aux')), axis=0)]
    psum x1 -> x0, waiting for transfers between devices: 280 us -> none  [on_device(): total = lax.psum(density, ('occ', 'aux'))]
  transfers between devices with their start and end apart: 3 -> 3, of which waited for: 3 -> 3; matrix products, arithmetic and copies ran while one was open for 11% -> 10% of each run, Pallas kernels for 0% -> 0%
where the time goes in v1:
time: 1560 us
  waiting for transfers between devices  913 us (59%)
  matrix products  211 us (14%)
  blocking collectives  188 us (12%)
  local copies, waits for them, and re-layouts  165 us (11%)
  loops' own time  42.8 us (3%)
  other arithmetic  23.5 us (2%)
    ppermute x2, waiting for transfers between devices, passed_along(): lax.ppermute(array, axis, [(i, (i + by) % count) for i in range(count)])  569 us
    all_gather x1, waiting for transfers between devices, on_device(): total = jnp.sum(lax.all_gather(density, ('occ', 'aux')), axis=0)  343 us
    all_to_all x1, blocking collectives, on_device(): lax.all_to_all(integrals, 'aux', split_axis=1, concat_axis=0, tiled=True)  188 us
    dot_general x16, matrix products, one_pair(): lax.dot_general(left, right, (((0,), (0,)), ((), ())), preferred_element_...  86.2 us
    dot_general x16, matrix products, one_pair(): lax.dot_general(right, amp, (((1,), (1,)), ((), ())), preferred_element_t...  77.5 us
    another operation x2, loops' own time, on_device(): gamma, density = lax.fori_loop(0, own, visit, (gamma, density))  42.8 us
    dynamic_slice x16, local copies, waits for them, and re-layouts, one_pair(): column = lax.dynamic_index_in_dim(grad_acc, slot, 1, False) + term  42.2 us
    dot_general x1, matrix products, transform(): jnp.dot(metric, moved.reshape(shape[0], -1), preferred_element_type=jnp.f...  38.5 us
  transfers between devices with their start and end apart: 3, of which 3 were waited for; matrix products, arithmetic and copies ran while one was open for 10% of the time, Pallas kernels for 0%

profile of v1, /device:TPU:0, one launch (start us, length us, event | category | flops | bytes accessed | tf_op | source)
XLA Modules:
  0.0 1559.7 jit_solution(4194682730207056767)
XLA Ops:
  7.2 12.0 copy.15
  19.3 187.7 %all_to_all.15 = bf16[512,32,512]{2,0,1:T(8,128)(2,1)S(1)} all-to-all(bf16[512,32,512]{2,0,1:T(8,128)(2,1)S(1)} %copy.15), channel_id=1, replica_groups=mesh['occ'=8,'aux'=4] {'aux'}, dimensions={1} | all-to-all | bytes 33554432 | tf_op jit(solution)/shard_map/all_to_all | solution.py:27
  206.9 38.4 %copy.16 = bf16[512,4,8,512]{3,2,0,1:T(8,128)(2,1)S(1)} copy(bf16[512,4,8,512]{3,0,2,1:T(8,128)(2,1)S(1)} %bitcast.110) | data formatting | bytes 33554432 | tf_op jit(solution)/shard_map/all_to_all | solution.py:27
  245.4 10.5 copy.23
  255.8 38.5 %convolution_convert_fusion = bf16[2048,4096]{1,0:T(8,128)(2,1)S(1)} fusion(bf16[2048,2048]{1,0:T(8,128)(2,1)S(1)} %bitcast.116, bf16[2048,4096]{1,0:T(8,128)(2,1)} %bitcast.113), kind=kOutput, calls=%fused_computation.42 | convolution fusion | flops 34368126976 | bytes 41943040 | tf_op jit(solution)/shard_map/dot_general | solution.py:17
  294.3 7.4 copy.27
  305.3 362.3 %collective-permute-done = bf16[2048,8,512]{2,0,1:T(8,128)(2,1)} collective-permute-done((bf16[2048,8,512]{2,0,1:T(8,128)(2,1)}, bf16[2048,8,512]{2,0,1:T(8,128)(2,1)}, u32[]{:S(2)}, u32[]{:S(2)}) %collective-permute-start) | collective-permute-done | bytes 16777248 | tf_op jit(solution)/shard_map/ppermute | solution.py:12
  667.5 11.3 broadcast_in_dim.27
  678.8 138.3 %while.37 = (s32[]{:T(128)}, f32[2048,8,512]{2,0,1:T(8,128)}, f32[512,512]{1,0:T(8,128)S(1)}, s32[8,2]{0,1:T(2,128)S(1)}, bf16[2048,8,512]{2,0,1:T(8,128)(2,1)},...) while((s32[]{:T(128)}, f32[2048,8,512]{2,0,1:T(8,128)}, ...), condition=%wide.region_1.2_spmd.clone, body=%wide.region_0.1_spmd.clone.sunk | while | flops 2419064832 | bytes 26745676 | solution.py:64
  682.6 5.4 fusion.79
  688.0 2.6 constant_dynamic-slice_fusion.12
  690.7 4.8 bitcast_dynamic-update-slice_fusion.5
  699.9 5.4 fusion.79
  705.3 2.6 constant_dynamic-slice_fusion.12
  708.0 4.9 bitcast_dynamic-update-slice_fusion.5
  717.2 5.4 fusion.79
  725.3 4.9 bitcast_dynamic-update-slice_fusion.5
  734.5 5.4 fusion.79
  742.6 4.8 bitcast_dynamic-update-slice_fusion.5
  751.8 5.4 fusion.79
  759.8 4.8 bitcast_dynamic-update-slice_fusion.5
  769.1 5.4 fusion.79
  777.1 4.9 bitcast_dynamic-update-slice_fusion.5
  786.4 5.4 fusion.79
  794.4 4.9 bitcast_dynamic-update-slice_fusion.5
  803.7 5.4 fusion.79
  811.7 4.8 bitcast_dynamic-update-slice_fusion.5
  817.2 206.8 %collective-permute-done.1 = bf16[2048,8,512]{2,0,1:T(8,128)(2,1)} collective-permute-done((bf16[2048,8,512]{2,0,1:T(8,128)(2,1)}, bf16[2048,8,512]{2,0,1:T(8,128)(2,1)}, u32[]{:S(2)}, u32[]{:S(2)}) %collective-permute-start.1) | collective-permute-done | bytes 16777248 | tf_op jit(solution)/shard_map/ppermute | solution.py:12
  1024.0 140.2 %while.36 = (s32[]{:T(128)}, f32[2048,8,512]{2,0,1:T(8,128)}, f32[512,512]{1,0:T(8,128)S(1)}, s32[8,2]{0,1:T(2,128)S(1)}, bf16[2048,8,512]{2,0,1:T(8,128)(2,1)},...) while((s32[]{:T(128)}, f32[2048,8,512]{2,0,1:T(8,128)}, ...), condition=%wide.region_3.4_spmd.clone, body=%wide.region_2.3_spmd.clone.sunk | while | flops 2418802688 | bytes 26745668 | solution.py:64
  1028.1 5.4 fusion.71
  1036.1 4.8 bitcast_dynamic-update-slice_fusion.4
  1045.6 5.4 fusion.71
  1053.7 4.9 bitcast_dynamic-update-slice_fusion.4
  1063.2 5.4 fusion.71
  1071.2 4.9 bitcast_dynamic-update-slice_fusion.4
  1080.7 5.4 fusion.71
  1088.7 4.8 bitcast_dynamic-update-slice_fusion.4
  1098.2 5.4 fusion.71
  1106.2 4.8 bitcast_dynamic-update-slice_fusion.4
  1115.7 5.4 fusion.71
  1123.7 4.9 bitcast_dynamic-update-slice_fusion.4
  1133.2 5.4 fusion.71
  1141.3 4.9 bitcast_dynamic-update-slice_fusion.4
  1150.8 5.4 fusion.71
  1158.8 4.8 bitcast_dynamic-update-slice_fusion.4
  1165.1 31.3 %copy.26 = bf16[2048,8,512]{2,1,0:T(8,128)(2,1)} copy(f32[2048,8,512]{2,0,1:T(8,128)} %get-tuple-element.518) | data formatting | bytes 50331648 | tf_op jit(solution)/shard_map/while | solution.py:64
  1196.4 343.5 %all-gather.3.cloned.1.call-done = f32[16384,512]{1,0:T(8,128)} async-done(((f32[512,512]{1,0:T(8,128)}), f32[16384,512]{1,0:T(8,128)}) %all-gather.3.cloned.1.call-update) | async-done | bytes 33554448 | tf_op jit(solution)/shard_map/all_gather | solution.py:65
  1539.9 12.3 reduce_sum.9
  (83 shorter events, 71.9 us)
Async XLA Ops:
  7.2 1532.7 %all-gather.3.cloned.1.call-start = ((), (), s32[]{:S(2)}) async-start(), calls=%async_computation.1 | async-start | bytes 34603008 | tf_op jit(solution)/shard_map/all_gather | solution.py:65
  206.9 48.9 %slice-start = ((s8[8388608]{0:T(1024)(128)(4,1)}), s8[4194304]{0:T(1024)(128)(4,1)S(1)}, s32[]{:S(2)}) async-start(s8[8388608]{0:T(1024)(128)(4,1)} %bitcast.115), calls=%async_computation.2 | async-start | bytes 8388608
  245.3 10.5 slice-start.1
  301.7 365.8 %collective-permute-start = (bf16[2048,8,512]{2,0,1:T(8,128)(2,1)}, bf16[2048,8,512]{2,0,1:T(8,128)(2,1)}, u32[]{:S(2)}, u32[]{:S(2)}) collective-permute-start(bf16[2048,8,512]{2,0,1:T(8,128)(2,1)} %bitcast.61), channel_id=1, source_target_pairs={{0,1},{1,2},{2,3},{3,4},{4,5},{5,6},{6,7},{7,8},{8,9},{9,10},{10,1... | collective-permute-start | bytes 50331656 | tf_op jit(solution)/shard_map/ppermute | solution.py:12
  302.7 721.3 %collective-permute-start.1 = (bf16[2048,8,512]{2,0,1:T(8,128)(2,1)}, bf16[2048,8,512]{2,0,1:T(8,128)(2,1)}, u32[]{:S(2)}, u32[]{:S(2)}) collective-permute-start(bf16[2048,8,512]{2,0,1:T(8,128)(2,1)} %bitcast.61), channel_id=1, source_target_pairs={{0,16},{1,17},{2,18},{3,19},{4,20},{5,21},{6,22},{7,23},{8,24},{9,... | collective-permute-start | bytes 50331656 | tf_op jit(solution)/shard_map/ppermute | solution.py:12
  305.2 373.5 %copy-start.1 = (f32[256]{0:T(256)S(1)}, f32[256]{0:T(256)}, u32[]{:S(2)}) copy-start(f32[256]{0:T(256)} %param.12) | copy-start | bytes 3076
  305.2 373.6 %copy-start.2 = (s32[8,2]{0,1:T(2,128)S(1)}, s32[8,2]{0,1:T(2,128)}, u32[]{:S(2)}) copy-start(s32[8,2]{0,1:T(2,128)} %param.14) | copy-start | bytes 196
  305.2 373.6 %copy-start.3 = (s32[8,2]{0,1:T(2,128)S(1)}, s32[8,2]{0,1:T(2,128)}, u32[]{:S(2)}) copy-start(s32[8,2]{0,1:T(2,128)} %param.15) | copy-start | bytes 196
  305.2 373.6 %copy-start.4 = (f32[512]{0:T(512)S(1)}, f32[512]{0:T(512)}, u32[]{:S(2)}) copy-start(f32[512]{0:T(512)} %param.13) | copy-start | bytes 6148
  1164.1 1.0 copy-start
Sparse Core Ops, SparseCore 0:
  1165.3 374.5 all-gather.2
